TPU v7x, 256 devices: a 8x8x2 block of a 8x8x16 slice. The times are simulated.
256 devices in a mesh: group: 2 (over z), dp: 16 (over y, core), tensor: 8 (over x).
Axes of the slice: x: 8, y: 8, z: 2, core: 2. Of those that a mesh axis runs over, the one named last changes fastest.
The devices are a block of a 8x8x16 slice.
Arguments:
- tokens: bfloat16 [4096, 5120], P(('group', 'dp'), 'tensor'), parts along dimension 0, may hold values from -6 to 6
- router: bfloat16 [5120, 8], replicated, may hold values from -0.078125 to 0.078125
- expert_gate: bfloat16 [5120, 32768], P(None, ('dp', 'tensor')), may hold values from -0.078125 to 0.078125
- expert_up: bfloat16 [5120, 32768], P(None, ('dp', 'tensor')), may hold values from -0.078125 to 0.078125
- expert_down: bfloat16 [32768, 5120], P(('dp', 'tensor')), may hold values from -0.09375 to 0.09375
- shared_gate: bfloat16 [5120, 4096], P('dp', 'tensor'), may hold values from -0.078125 to 0.078125
- shared_up: bfloat16 [5120, 4096], P('dp', 'tensor'), may hold values from -0.078125 to 0.078125
- shared_down: bfloat16 [4096, 5120], P('tensor', 'dp'), may hold values from -0.09375 to 0.09375
- expert_ids: int32 [4096], P(('group', 'dp')), parts along dimension 0, may hold values from 0 to 7, as said below
- expert_slots: int32 [4096], P(('group', 'dp')), parts along dimension 0, may hold values from 0 to 31, as said below
Outputs:
- mixed: bfloat16 [4096, 5120], P(('group', 'dp'), 'tensor'), parts along dimension 0
There are 2 independent parts, one for each index of `group`. A program takes and returns all parts, laid end to end along the dimension named above; an argument that names none is the same for every part. Nothing has to cross between parts.
Inputs may be any that keep to these rules, and one draw needn't show every extreme that they name: `expert_ids`: among the tokens of one index of dp no expert has more than 32; in every draw one expert has exactly 32 tokens from every index of dp. `expert_slots`: tokens of one index of dp with the same expert have distinct slots.
All inputs are finite; a program needn't handle non-finite values.
Results may differ from a plain program's by a relative error of at most 0.015.
Values may be sent and summed in bfloat16 or wider, within the bound.
No kernel may reach another device: no remote copies, remote signals or barrier semaphores. Data moves between devices by JAX's collectives and lax.ppermute only.
A program may use at most 128 MiB of HBM per device.

v0:
```python
import jax
import jax.numpy as jnp
from jax import lax
from jax.sharding import PartitionSpec as P


def joined_along(tiles, dim):
    dims = list(tiles.shape[1:])
    dims[dim] *= tiles.shape[0]
    return jnp.moveaxis(tiles, 0, dim).reshape(dims)


def copy_for_each(value, axis):
    copies = jnp.broadcast_to(value, (lax.axis_size(axis), *value.shape))
    return lax.all_to_all(copies, axis, split_axis=0, concat_axis=0, tiled=True)


def gather_directly(value, axis, dim):
    return joined_along(copy_for_each(value, axis), dim)


def side_by_side(arrays, axis, dim, along):
    both = jnp.concatenate(arrays, axis=along)
    out, at, finished = (lax.all_gather(both, axis, axis=dim, tiled=True), 0, [])
    for a in arrays:
        finished.append(lax.slice_in_dim(out, at, at + a.shape[along], axis=along))
        at += a.shape[along]
    return tuple(finished)


def split_up(value, dim, devices):
    before, after = (value.shape[:dim], value.shape[dim + 1 :])
    return jnp.moveaxis(value.reshape(*before, devices, -1, *after), dim, 0)


def sum_at_owner(value, axis, dim):
    tiles = split_up(value, dim, lax.axis_size(axis))
    arrived = lax.all_to_all(tiles, axis, split_axis=0, concat_axis=0, tiled=True)
    return arrived.astype(jnp.float32).sum(axis=0)


def swapped(value, axis, bit):
    mask = 2**bit
    pairs = [(source, source ^ mask) for source in range(lax.axis_size(axis))]
    return lax.ppermute(value, axis, pairs)


def on_device(
    tokens,
    router,
    expert_gate,
    expert_up,
    expert_down,
    shared_gate,
    shared_up,
    shared_down,
    expert_ids,
    expert_slots,
):
    tok_rows, part_width = tokens.shape
    dp_count = lax.axis_size("dp")
    experts = dp_count // 2
    capacity = min(2 * tok_rows // experts, tok_rows // 2)
    gathered = gather_directly(tokens, "tensor", 1)
    logits = jnp.dot(gathered, router, preferred_element_type=jnp.float32)
    one_hot = (expert_ids[:, None] == jnp.arange(experts, dtype=jnp.int32)[None, :]).astype(
        jnp.float32
    )
    gating = jax.nn.sigmoid(jnp.sum(logits * one_hot, axis=1))
    routed = (tokens.astype(jnp.float32) * gating[:, None]).astype(jnp.bfloat16)
    outgoing = (
        jnp.zeros((experts, capacity, part_width), jnp.bfloat16)
        .at[expert_ids, expert_slots]
        .set(routed)
    )
    pieces = side_by_side((shared_gate, shared_up), "dp", 0, 1)
    gate_sum = jnp.dot(gathered, pieces[0], preferred_element_type=jnp.float32)
    up_sum = jnp.dot(gathered, pieces[1], preferred_element_type=jnp.float32)
    shared_hidden = (jax.nn.silu(gate_sum) * up_sum).astype(jnp.bfloat16)
    shared_terms = jnp.dot(
        shared_hidden,
        lax.all_gather(shared_down, "dp", axis=1, tiled=True),
        preferred_element_type=jnp.float32,
    )
    shared_out = lax.psum_scatter(
        shared_terms.astype(jnp.bfloat16), "tensor", scatter_dimension=1, tiled=True
    ).astype(jnp.float32)
    half_cap = capacity // 2
    to_send = outgoing.reshape(dp_count, half_cap, part_width)
    own_half = lax.all_to_all(to_send, "dp", split_axis=0, concat_axis=0, tiled=True)
    partner = swapped(own_half, "dp", 0)
    parity = lax.axis_index("dp") % 2
    odd_host = parity == 1
    lower_half = jnp.where(odd_host, partner, own_half)
    upper_half = jnp.where(odd_host, own_half, partner)
    received = jnp.concatenate([lower_half, upper_half], axis=1)
    source_count = received.shape[0]
    slot_count = received.shape[1]
    slot_total = source_count * slot_count
    portion = lax.all_gather(received, "tensor", axis=2, tiled=True)
    flattened = portion.reshape(slot_total, portion.shape[2])
    gate_e = jnp.dot(flattened, expert_gate, preferred_element_type=jnp.float32)
    up_e = jnp.dot(flattened, expert_up, preferred_element_type=jnp.float32)
    hidden_e = (jax.nn.silu(gate_e) * up_e).astype(jnp.bfloat16)
    expert_terms = jnp.dot(hidden_e, expert_down, preferred_element_type=jnp.float32)
    expert_terms = expert_terms.reshape(source_count, slot_count, expert_terms.shape[1])
    partials = sum_at_owner(expert_terms.astype(jnp.bfloat16), "tensor", 2)
    partner_sum = swapped(partials.astype(jnp.bfloat16), "dp", 0).astype(partials.dtype)
    paired = partials + partner_sum
    kept_half = lax.dynamic_slice_in_dim(paired, parity * half_cap, half_cap, 1).astype(
        jnp.bfloat16
    )
    returned_raw = lax.all_to_all(kept_half, "dp", split_axis=0, concat_axis=0, tiled=True)
    returned = returned_raw.reshape(experts, capacity, part_width)
    expert_out = returned[expert_ids, expert_slots]
    return (shared_out + expert_out.astype(jnp.float32)).astype(jnp.bfloat16)


def solution(mesh):
    in_specs = (
        P(("group", "dp"), "tensor"),
        P(),
        P(None, ("dp", "tensor")),
        P(None, ("dp", "tensor")),
        P(("dp", "tensor"), None),
        P("dp", "tensor"),
        P("dp", "tensor"),
        P("tensor", "dp"),
        P(("group", "dp")),
        P(("group", "dp")),
    )
    out_specs = P(("group", "dp"), "tensor")
    return jax.shard_map(
        on_device, mesh=mesh, in_specs=in_specs, out_specs=out_specs, check_vma=False
    )
```

profile of v0, /device:TPU:515, one launch (start us, length us, event | category | flops | bytes accessed | tf_op | source)
XLA Modules:
  0.0 342.5 jit_solution(5509344661017308061)
XLA Ops:
  9.0 7.2 %all-to-all-start = ((bf16[8,128,640]{1,2,0:T(8,128)(2,1)}), bf16[8,128,640]{1,2,0:T(8,128)(2,1)}, u32[]{:S(2)}, u32[]{:S(2)}) async-start(bf16[8,128,640]{1,2,0:T(8,128)(2,1)} %broadcast_in_dim.8), calls=%async_computation | async-start | bytes 2621440 | tf_op jit(solution)/shard_map/all_to_all | solution.py:15
  16.2 19.5 %all-to-all-done = bf16[8,128,640]{1,2,0:T(8,128)(2,1)} async-done(((bf16[8,128,640]{1,2,0:T(8,128)(2,1)}), bf16[8,128,640]{1,2,0:T(8,128)(2,1)}, u32[]{:S(2)}, u32[]{:S(2)}) %all-to-all-start) | async-done | bytes 1310752 | tf_op jit(solution)/shard_map/all_to_all | solution.py:15
  37.5 8.0 %scatter_fusion = bf16[8,32,640]{2,1,0:T(8,128)(2,1)S(1)} fusion(bf16[8,32,640]{2,1,0:T(8,128)(2,1)S(1)} %broadcast_in_dim.18, s32[128]{0:T(128)S(1)} %get-tuple-element.8, bf16[128,640]{1,0:T(8,128)(2,1)S(1)} %multiply_convert_fusion), kind=kCustom, calls=%fused_computation.1 | custom fusion | bytes 492544 | tf_op jit(solution)/shard_map/scatter | solution.py:74
  45.5 40.7 %all_to_all.20 = bf16[16,16,640]{2,1,0:T(8,128)(2,1)S(1)} all-to-all(bf16[16,16,640]{2,1,0:T(8,128)(2,1)S(1)} %bitcast.60), channel_id=1, replica_groups=mesh['group'=2,'dp'=16,'tensor'=8] {'dp'}, dimensions={0} | all-to-all | bytes 655360 | tf_op jit(solution)/shard_map/all_to_all | solution.py:90
  86.2 1.6 collective-permute-done
  88.9 2.0 pad_maximum_fusion
  91.7 63.9 %all-gather.8.cloned.1.call-done = bf16[16,32,5120]{2,1,0:T(8,128)(2,1)} async-done(((bf16[16,32,640]{2,1,0:T(8,128)(2,1)}), bf16[16,32,5120]{2,1,0:T(8,128)(2,1)}) %all-gather.8.cloned.1.call-update) | async-done | bytes 5242896 | tf_op jit(solution)/shard_map/all_gather | solution.py:100
  155.6 4.8 %fusion.40 = f32[512,256]{1,0:T(8,128)S(1)} fusion(bf16[512,5120]{1,0:T(8,128)(2,1)} %bitcast.65, bf16[5120,256]{1,0:T(8,128)(2,1)} %param.12), kind=kOutput, calls=%fused_computation.52 | convolution fusion | flops 1342177280 | bytes 8388608 | tf_op jit(solution)/shard_map/dot_general | solution.py:102
  160.5 11.2 %convolution_convert_fusion = bf16[512,5120]{1,0:T(8,128)(2,1)} fusion(bf16[256,5120]{1,0:T(8,128)(2,1)S(1)} %copy-done, bf16[512,5120]{1,0:T(8,128)(2,1)} %bitcast.66, bf16[5120,256]{1,0:T(8,128)(2,1)} %param.13, f32[512,256]{1,0:T(8,128)S(1)} %fusion.40), kind=kOutput, calls=%fused_computation.3 | convolution fusion | flops 2687762432 | bytes 16252928 | tf_op jit(solution)/shard_map/dot_general | solution.py:105
  171.7 3.7 %copy.16 = bf16[64,8,8,640]{3,2,1,0:T(8,128)(2,1)S(1)} copy(bf16[64,8,8,640]{3,1,2,0:T(8,128)(2,1)} %bitcast.62) | data formatting | bytes 10485760
  175.3 3.1 copy.18
  178.4 6.2 %all-to-all-start.2 = ((bf16[8,16,32,640]{3,2,1,0:T(8,128)(2,1)}), bf16[8,16,32,640]{3,2,1,0:T(8,128)(2,1)}, u32[]{:S(2)}, u32[]{:S(2)}) async-start(bf16[8,16,32,640]{3,2,1,0:T(8,128)(2,1)} %bitcast.58), calls=%async_computation.2 | async-start | bytes 10485760 | tf_op jit(solution)/shard_map/all_to_all | solution.py:38
  184.6 41.0 %all-gather.4.cloned.1.call-done = bf16[5120,1024]{1,0:T(8,128)(2,1)} async-done(((bf16[320,1024]{1,0:T(8,128)(2,1)}), bf16[5120,1024]{1,0:T(8,128)(2,1)}) %all-gather.4.cloned.1.call-update) | async-done | bytes 10485776 | tf_op jit(solution)/shard_map/all_gather | solution.py:24
  225.6 4.4 %fusion.5 = f32[128,512]{0,1:T(8,128)S(1)} fusion(bf16[128,5120]{0,1:T(8,128)(2,1)} %bitcast.1, bf16[5120,1024]{1,0:T(8,128)(2,1)} %all-gather.4.cloned.1.call-done), kind=kOutput, calls=%fused_computation.12 | convolution fusion | flops 671088640 | bytes 6815744 | tf_op jit(solution)/shard_map/dot_general | solution.py:77
  230.1 40.7 %all-gather.6.cloned.1.call-done = bf16[512,5120]{0,1:T(8,128)(2,1)} async-done(((bf16[512,320]{0,1:T(8,128)(2,1)}), bf16[512,5120]{0,1:T(8,128)(2,1)}) %all-gather.6.cloned.1.call-update) | async-done | bytes 5242896 | tf_op jit(solution)/shard_map/all_gather | solution.py:82
  270.7 11.2 %convolution_convert_fusion.1 = bf16[128,5120]{1,0:T(8,128)(2,1)} fusion(bf16[512,5120]{0,1:T(8,128)(2,1)} %all-gather.6.cloned.1.call-done, bf16[128,5120]{0,1:T(8,128)(2,1)} %bitcast.1, bf16[5120,1024]{1,0:T(8,128)(2,1)} %all-gather.4.cloned.1.call-done, f32[128,512]{0,1:T(8,128)S(1)} %fusion.5), kind=kOutput, calls=%fused_computation.4 | convolution fusion | flops 1343225856 | bytes 13369344 | tf_op jit(solution)/shard_map/dot_general | solution.py:80
  281.9 2.4 copy.14
  284.4 17.9 %all-to-all-done.2 = bf16[8,16,32,640]{3,2,1,0:T(8,128)(2,1)} async-done(((bf16[8,16,32,640]{3,2,1,0:T(8,128)(2,1)}), bf16[8,16,32,640]{3,2,1,0:T(8,128)(2,1)}, u32[]{:S(2)}, u32[]{:S(2)}) %all-to-all-start.2) | async-done | bytes 5242912 | tf_op jit(solution)/shard_map/all_to_all | solution.py:38
  302.4 3.4 %convert_reduce_fusion = f32[16,32,640]{2,1,0:T(8,128)S(1)} fusion(bf16[8,16,32,640]{3,2,1,0:T(8,128)(2,1)} %all-to-all-done.2), kind=kLoop, calls=%fused_computation.2 | loop fusion | flops 4915200 | bytes 6553600 | tf_op jit(solution)/shard_map/reduce_sum | solution.py:39
  307.0 2.7 collective-permute-start.1
  309.7 1.9 collective-permute-done.1
  311.5 2.0 fusion.20
  313.5 7.4 %all-to-all-start.3 = ((bf16[16,16,640]{2,1,0:T(8,128)(2,1)}), bf16[16,16,640]{2,1,0:T(8,128)(2,1)S(1)}, u32[]{:S(2)}, u32[]{:S(2)}) async-start(bf16[16,16,640]{2,1,0:T(8,128)(2,1)} %fusion.20), calls=%async_computation.3 | async-start | bytes 655360 | tf_op jit(solution)/shard_map/all_to_all | solution.py:113
  322.0 11.9 %all-to-all-done.3 = bf16[16,16,640]{2,1,0:T(8,128)(2,1)S(1)} async-done(((bf16[16,16,640]{2,1,0:T(8,128)(2,1)}), bf16[16,16,640]{2,1,0:T(8,128)(2,1)S(1)}, u32[]{:S(2)}, u32[]{:S(2)}) %all-to-all-start.3) | async-done | bytes 327712 | tf_op jit(solution)/shard_map/all_to_all | solution.py:113
  (35 shorter events, 10.6 us)
Async XLA Ops:
  6.5 153.9 %copy-start = (bf16[256,5120]{1,0:T(8,128)(2,1)S(1)}, bf16[256,5120]{1,0:T(8,128)(2,1)}, u32[]{:S(2)}) copy-start(bf16[256,5120]{1,0:T(8,128)(2,1)} %param.14) | copy-start | bytes 7864324
  6.6 9.7 %copy-start.4 = (s32[128]{0:T(128)S(1)}, s32[128]{0:T(128)}, u32[]{:S(2)}) copy-start(s32[128]{0:T(128)} %param.18) | copy-start | bytes 1540
  6.6 9.7 %copy-start.5 = (s32[128]{0:T(128)S(1)}, s32[128]{0:T(128)}, u32[]{:S(2)}) copy-start(s32[128]{0:T(128)} %param.19) | copy-start | bytes 1540
  6.6 29.1 %copy-start.3 = (bf16[5120,8]{0,1:T(8,128)(2,1)S(1)}, bf16[5120,8]{0,1:T(8,128)(2,1)}, u32[]{:S(2)}) copy-start(bf16[5120,8]{0,1:T(8,128)(2,1)} %param.11) | copy-start | bytes 245764
  7.8 29.5 %copy-start.2 = (bf16[128,640]{1,0:T(8,128)(2,1)S(1)}, bf16[128,640]{1,0:T(8,128)(2,1)}, u32[]{:S(2)}) copy-start(bf16[128,640]{1,0:T(8,128)(2,1)} %param.10) | copy-start | bytes 491524
  9.0 26.6 %all-to-all-start = ((bf16[8,128,640]{1,2,0:T(8,128)(2,1)}), bf16[8,128,640]{1,2,0:T(8,128)(2,1)}, u32[]{:S(2)}, u32[]{:S(2)}) async-start(bf16[8,128,640]{1,2,0:T(8,128)(2,1)} %broadcast_in_dim.8), calls=%async_computation | async-start | bytes 2621440 | tf_op jit(solution)/shard_map/all_to_all | solution.py:15
  16.2 139.4 %all-gather.8.cloned.1.call-start = ((), (), s32[]{:S(2)}) async-start(), calls=%async_computation.7 | async-start | bytes 5898240 | tf_op jit(solution)/shard_map/all_gather | solution.py:100
  86.2 1.6 collective-permute-start
  88.8 136.8 %all-gather.4.cloned.1.call-start = ((), (), s32[]{:S(2)}) async-start(), calls=%async_computation.5 | async-start | bytes 11141120 | tf_op jit(solution)/shard_map/all_gather | solution.py:24
  90.9 179.8 %all-gather.6.cloned.1.call-start = ((), (), s32[]{:S(2)}) async-start(), calls=%async_computation.6 | async-start | bytes 5570560 | tf_op jit(solution)/shard_map/all_gather | solution.py:82
  178.4 124.0 %all-to-all-start.2 = ((bf16[8,16,32,640]{3,2,1,0:T(8,128)(2,1)}), bf16[8,16,32,640]{3,2,1,0:T(8,128)(2,1)}, u32[]{:S(2)}, u32[]{:S(2)}) async-start(bf16[8,16,32,640]{3,2,1,0:T(8,128)(2,1)} %bitcast.58), calls=%async_computation.2 | async-start | bytes 10485760 | tf_op jit(solution)/shard_map/all_to_all | solution.py:38
  184.6 136.3 %reduce-scatter.4.cloned.1.call-start = ((), (), s32[]{:S(2)}) async-start(), calls=%async_computation.8 | async-start | bytes 1474560
  305.8 1.1 copy-start.1
  307.0 4.6 %collective-permute-start.1 = (bf16[16,32,640]{2,1,0:T(8,128)(2,1)S(1)}, bf16[16,32,640]{2,1,0:T(8,128)(2,1)}, u32[]{:S(2)}, u32[]{:S(2)}) collective-permute-start(bf16[16,32,640]{2,1,0:T(8,128)(2,1)S(1)} %convert_element_type.53), channel_id=1, source_target_pairs={{0,8},{8,0},{16,24},{24,16},{32,40},{40,32},{48,56},{56,48},{64,72... | collective-permute-start | bytes 1966088 | tf_op jit(solution)/shard_map/ppermute | solution.py:45
  313.5 20.4 %all-to-all-start.3 = ((bf16[16,16,640]{2,1,0:T(8,128)(2,1)}), bf16[16,16,640]{2,1,0:T(8,128)(2,1)S(1)}, u32[]{:S(2)}, u32[]{:S(2)}) async-start(bf16[16,16,640]{2,1,0:T(8,128)(2,1)} %fusion.20), calls=%async_computation.3 | async-start | bytes 655360 | tf_op jit(solution)/shard_map/all_to_all | solution.py:113
Sparse Core Ops, SparseCore 0:
  88.9 66.6 all-gather.7
  157.5 68.1 all-gather.3
  227.5 43.1 all-gather.5
  284.5 36.2 reduce-scatter.3
where the time goes:
time: 343 us
  waiting for transfers between devices  199 us (58%)
  blocking collectives  40.7 us (12%)
  matrix products  33.2 us (10%)
  starting transfers between devices  23.6 us (7%)
  local copies, waits for them, and re-layouts  23.2 us (7%)
  between operations  13.3 us (4%)
  other arithmetic  9.27 us (3%)
    all_gather x1, waiting for transfers between devices, on_device(): portion = lax.all_gather(received, 'tensor', axis=2, tiled=True)  63.9 us
    all_gather x1, waiting for transfers between devices, side_by_side(): lax.all_gather(both, axis, axis=dim, tiled=True)  41 us
    all_to_all x1, blocking collectives, on_device(): lax.all_to_all(to_send, 'dp', split_axis=0, concat_axis=0, tiled=True)  40.7 us
    all_gather x1, waiting for transfers between devices, on_device(): lax.all_gather(shared_down, 'dp', axis=1, tiled=True)  40.7 us
    all_to_all x1, waiting for transfers between devices, copy_for_each(): return lax.all_to_all(copies, axis, split_axis=0, concat_axis=0, tiled=True)  19.5 us
    all_to_all x1, waiting for transfers between devices, sum_at_owner(): lax.all_to_all(tiles, axis, split_axis=0, concat_axis=0, tiled=True)  17.9 us
    all_to_all x1, waiting for transfers between devices, on_device(): lax.all_to_all(kept_half, 'dp', split_axis=0, concat_axis=0, tiled=True)  11.9 us
    dot_general x1, matrix products, on_device(): jnp.dot(hidden_e, expert_down, preferred_element_type=jnp.float32)  11.2 us
  transfers between devices with their start and end apart: 9, of which 8 were waited for; matrix products, arithmetic and copies ran while one was open for 14% of the time, Pallas kernels for 0%

commit v1 on v0

--- a/solution.py
+++ b/solution.py
@@ -97,7 +97,7 @@
     source_count = received.shape[0]
     slot_count = received.shape[1]
     slot_total = source_count * slot_count
-    portion = lax.all_gather(received, "tensor", axis=2, tiled=True)
+    portion = jnp.concatenate(lax.all_gather(received, "tensor"), axis=2)
     flattened = portion.reshape(slot_total, portion.shape[2])
     gate_e = jnp.dot(flattened, expert_gate, preferred_element_type=jnp.float32)
     up_e = jnp.dot(flattened, expert_up, preferred_element_type=jnp.float32)

time: 343 us -> 353 us (1.029)
  local copies, waits for them, and re-layouts: 23.2 us -> 31.3 us
  waiting for transfers between devices: 199 us -> 205 us
  matrix products: 33.2 us -> 28.9 us
    all_to_all x1, waiting for transfers between devices: 17.9 us -> 29.7 us  [sum_at_owner(): lax.all_to_all(tiles, axis, split_axis=0, concat_axis=0, tiled=True)]
    all_gather x1, waiting for transfers between devices: 41 us -> 35.3 us  [side_by_side(): lax.all_gather(both, axis, axis=dim, tiled=True)]
    reshape x0 -> x1, local copies, waits for them, and re-layouts: none -> 5.51 us  [on_device(): portion = jnp.concatenate(lax.all_gather(received, 'tensor'), axis=2)]
    unnamed x16 -> x23, local copies, waits for them, and re-layouts: 9.48 us -> 12 us
where the time goes in v1:
time: 353 us; the launch traced here: 352 us
  waiting for transfers between devices  205 us (58%)
  blocking collectives  40.7 us (12%)
  local copies, waits for them, and re-layouts  31.3 us (9%)
  matrix products  28.9 us (8%)
  starting transfers between devices  24 us (7%)
  between operations  13.3 us (4%)
  other arithmetic  9.23 us (3%)
    all_gather x1, waiting for transfers between devices, on_device(): portion = jnp.concatenate(lax.all_gather(received, 'tensor'), axis=2)  63.9 us
    all_gather x1, waiting for transfers between devices, on_device(): lax.all_gather(shared_down, 'dp', axis=1, tiled=True)  40.7 us
    all_to_all x1, blocking collectives, on_device(): lax.all_to_all(to_send, 'dp', split_axis=0, concat_axis=0, tiled=True)  40.7 us
    all_gather x1, waiting for transfers between devices, side_by_side(): lax.all_gather(both, axis, axis=dim, tiled=True)  35.3 us
    all_to_all x1, waiting for transfers between devices, sum_at_owner(): lax.all_to_all(tiles, axis, split_axis=0, concat_axis=0, tiled=True)  29.7 us
    all_to_all x1, waiting for transfers between devices, copy_for_each(): return lax.all_to_all(copies, axis, split_axis=0, concat_axis=0, tiled=True)  19.5 us
    unnamed x23, local copies, waits for them, and re-layouts  12 us
    all_to_all x1, waiting for transfers between devices, on_device(): lax.all_to_all(kept_half, 'dp', split_axis=0, concat_axis=0, tiled=True)  11.9 us
  transfers between devices with their start and end apart: 9, of which 8 were waited for; matrix products, arithmetic and copies ran while one was open for 14% of the time, Pallas kernels for 0%

profile of v1, /device:TPU:515, one launch (start us, length us, event | category | flops | bytes accessed | tf_op | source)
XLA Modules:
  0.0 352.5 jit_solution(10060051998539844284)
XLA Ops:
  9.1 7.2 %all-to-all-start = ((bf16[8,128,640]{1,2,0:T(8,128)(2,1)}), bf16[8,128,640]{1,2,0:T(8,128)(2,1)}, u32[]{:S(2)}, u32[]{:S(2)}) async-start(bf16[8,128,640]{1,2,0:T(8,128)(2,1)} %broadcast_in_dim.8), calls=%async_computation | async-start | bytes 2621440 | tf_op jit(solution)/shard_map/all_to_all | solution.py:15
  16.2 19.5 %all-to-all-done = bf16[8,128,640]{1,2,0:T(8,128)(2,1)} async-done(((bf16[8,128,640]{1,2,0:T(8,128)(2,1)}), bf16[8,128,640]{1,2,0:T(8,128)(2,1)}, u32[]{:S(2)}, u32[]{:S(2)}) %all-to-all-start) | async-done | bytes 1310752 | tf_op jit(solution)/shard_map/all_to_all | solution.py:15
  37.5 8.0 %scatter_fusion = bf16[8,32,640]{2,1,0:T(8,128)(2,1)S(1)} fusion(bf16[8,32,640]{2,1,0:T(8,128)(2,1)S(1)} %broadcast_in_dim.18, s32[128]{0:T(128)S(1)} %get-tuple-element.8, bf16[128,640]{1,0:T(8,128)(2,1)S(1)} %multiply_convert_fusion), kind=kCustom, calls=%fused_computation.1 | custom fusion | bytes 492544 | tf_op jit(solution)/shard_map/scatter | solution.py:74
  45.5 40.7 %all_to_all.20 = bf16[16,16,640]{2,1,0:T(8,128)(2,1)S(1)} all-to-all(bf16[16,16,640]{2,1,0:T(8,128)(2,1)S(1)} %bitcast.66), channel_id=1, replica_groups=mesh['group'=2,'dp'=16,'tensor'=8] {'dp'}, dimensions={0} | all-to-all | bytes 655360 | tf_op jit(solution)/shard_map/all_to_all | solution.py:90
  86.2 1.6 collective-permute-done
  88.9 2.0 pad_maximum_fusion
  91.7 63.9 %all-gather.9.cloned.1.call-done = bf16[128,32,640]{2,1,0:T(8,128)(2,1)} async-done(((bf16[16,32,640]{2,1,0:T(8,128)(2,1)}), bf16[128,32,640]{2,1,0:T(8,128)(2,1)}) %all-gather.9.cloned.1.call-update) | async-done | bytes 5242896 | tf_op jit(solution)/shard_map/all_gather | solution.py:100
  155.6 5.5 %copy.15 = bf16[16,32,8,640]{3,2,1,0:T(8,128)(2,1)S(1)} copy(bf16[16,32,8,640]{3,1,0,2:T(8,128)(2,1)} %bitcast.68) | data formatting | bytes 10485760 | tf_op jit(solution)/shard_map/reshape | solution.py:100
  162.3 2.3 copy-done.3
  166.1 11.2 %convolution_convert_fusion = bf16[512,5120]{1,0:T(8,128)(2,1)} fusion(bf16[256,5120]{1,0:T(8,128)(2,1)S(1)} %copy-done, bf16[512,5120]{1,0:T(8,128)(2,1)} %bitcast.70, bf16[5120,256]{1,0:T(8,128)(2,1)} %param.13, f32[512,256]{1,0:T(8,128)S(1)} %fusion.40), kind=kOutput, calls=%fused_computation.3 | convolution fusion | flops 2687762432 | bytes 16252928 | tf_op jit(solution)/shard_map/dot_general | solution.py:105
  177.3 3.8 %copy.20 = bf16[64,8,8,640]{3,2,1,0:T(8,128)(2,1)S(1)} copy(bf16[64,8,8,640]{3,1,2,0:T(8,128)(2,1)} %bitcast.71) | data formatting | bytes 10485760
  181.1 3.1 copy.22
  184.2 6.2 %all-to-all-start.2 = ((bf16[8,16,32,640]{3,2,1,0:T(8,128)(2,1)}), bf16[8,16,32,640]{3,2,1,0:T(8,128)(2,1)}, u32[]{:S(2)}, u32[]{:S(2)}) async-start(bf16[8,16,32,640]{3,2,1,0:T(8,128)(2,1)} %bitcast.63), calls=%async_computation.2 | async-start | bytes 10485760 | tf_op jit(solution)/shard_map/all_to_all | solution.py:38
  190.4 35.3 %all-gather.5.cloned.1.call-done = bf16[5120,1024]{1,0:T(8,128)(2,1)} async-done(((bf16[320,1024]{1,0:T(8,128)(2,1)}), bf16[5120,1024]{1,0:T(8,128)(2,1)}) %all-gather.5.cloned.1.call-update) | async-done | bytes 10485776 | tf_op jit(solution)/shard_map/all_gather | solution.py:24
  225.7 4.4 %fusion.5 = f32[128,512]{0,1:T(8,128)S(1)} fusion(bf16[128,5120]{0,1:T(8,128)(2,1)} %bitcast.1, bf16[5120,1024]{1,0:T(8,128)(2,1)} %all-gather.5.cloned.1.call-done), kind=kOutput, calls=%fused_computation.12 | convolution fusion | flops 671088640 | bytes 6815744 | tf_op jit(solution)/shard_map/dot_general | solution.py:77
  230.1 40.7 %all-gather.7.cloned.1.call-done = bf16[512,5120]{0,1:T(8,128)(2,1)} async-done(((bf16[512,320]{0,1:T(8,128)(2,1)}), bf16[512,5120]{0,1:T(8,128)(2,1)}) %all-gather.7.cloned.1.call-update) | async-done | bytes 5242896 | tf_op jit(solution)/shard_map/all_gather | solution.py:82
  270.8 10.1 %convolution_convert_fusion.1 = bf16[128,5120]{1,0:T(8,128)(2,1)S(1)} fusion(bf16[512,5120]{0,1:T(8,128)(2,1)} %all-gather.7.cloned.1.call-done, bf16[128,5120]{0,1:T(8,128)(2,1)} %bitcast.1, bf16[5120,1024]{1,0:T(8,128)(2,1)} %all-gather.5.cloned.1.call-done, f32[128,512]{0,1:T(8,128)S(1)} %fusion.5), kind=kOutput, calls=%fused_computation.4 | convolution fusion | flops 1343225856 | bytes 13369344 | tf_op jit(solution)/shard_map/dot_general | solution.py:80
  282.4 29.7 %all-to-all-done.2 = bf16[8,16,32,640]{3,2,1,0:T(8,128)(2,1)} async-done(((bf16[8,16,32,640]{3,2,1,0:T(8,128)(2,1)}), bf16[8,16,32,640]{3,2,1,0:T(8,128)(2,1)}, u32[]{:S(2)}, u32[]{:S(2)}) %all-to-all-start.2) | async-done | bytes 5242912 | tf_op jit(solution)/shard_map/all_to_all | solution.py:38
  312.2 3.4 convert_reduce_fusion
  316.7 2.9 collective-permute-start.1
  319.6 1.9 collective-permute-done.1
  321.4 1.9 fusion.20
  323.4 7.5 %all-to-all-start.3 = ((bf16[16,16,640]{2,1,0:T(8,128)(2,1)}), bf16[16,16,640]{2,1,0:T(8,128)(2,1)S(1)}, u32[]{:S(2)}, u32[]{:S(2)}) async-start(bf16[16,16,640]{2,1,0:T(8,128)(2,1)} %fusion.20), calls=%async_computation.3 | async-start | bytes 655360 | tf_op jit(solution)/shard_map/all_to_all | solution.py:113
  332.0 11.9 %all-to-all-done.3 = bf16[16,16,640]{2,1,0:T(8,128)(2,1)S(1)} async-done(((bf16[16,16,640]{2,1,0:T(8,128)(2,1)}), bf16[16,16,640]{2,1,0:T(8,128)(2,1)S(1)}, u32[]{:S(2)}, u32[]{:S(2)}) %all-to-all-start.3) | async-done | bytes 327712 | tf_op jit(solution)/shard_map/all_to_all | solution.py:113
  (43 shorter events, 14.7 us)
Async XLA Ops:
  6.5 159.6 %copy-start = (bf16[256,5120]{1,0:T(8,128)(2,1)S(1)}, bf16[256,5120]{1,0:T(8,128)(2,1)}, u32[]{:S(2)}) copy-start(bf16[256,5120]{1,0:T(8,128)(2,1)} %param.14) | copy-start | bytes 7864324
  6.6 9.7 %copy-start.6 = (s32[128]{0:T(128)S(1)}, s32[128]{0:T(128)}, u32[]{:S(2)}) copy-start(s32[128]{0:T(128)} %param.18) | copy-start | bytes 1540
  6.6 9.7 %copy-start.7 = (s32[128]{0:T(128)S(1)}, s32[128]{0:T(128)}, u32[]{:S(2)}) copy-start(s32[128]{0:T(128)} %param.19) | copy-start | bytes 1540
  6.6 29.2 %copy-start.5 = (bf16[5120,8]{0,1:T(8,128)(2,1)S(1)}, bf16[5120,8]{0,1:T(8,128)(2,1)}, u32[]{:S(2)}) copy-start(bf16[5120,8]{0,1:T(8,128)(2,1)} %param.11) | copy-start | bytes 245764
  7.8 29.5 %copy-start.4 = (bf16[128,640]{1,0:T(8,128)(2,1)S(1)}, bf16[128,640]{1,0:T(8,128)(2,1)}, u32[]{:S(2)}) copy-start(bf16[128,640]{1,0:T(8,128)(2,1)} %param.10) | copy-start | bytes 491524
  9.1 26.6 %all-to-all-start = ((bf16[8,128,640]{1,2,0:T(8,128)(2,1)}), bf16[8,128,640]{1,2,0:T(8,128)(2,1)}, u32[]{:S(2)}, u32[]{:S(2)}) async-start(bf16[8,128,640]{1,2,0:T(8,128)(2,1)} %broadcast_in_dim.8), calls=%async_computation | async-start | bytes 2621440 | tf_op jit(solution)/shard_map/all_to_all | solution.py:15
  16.2 139.4 %all-gather.9.cloned.1.call-start = ((), (), s32[]{:S(2)}) async-start(), calls=%async_computation.7 | async-start | bytes 5898240 | tf_op jit(solution)/shard_map/all_gather | solution.py:100
  86.2 1.6 collective-permute-start
  88.8 136.8 %all-gather.5.cloned.1.call-start = ((), (), s32[]{:S(2)}) async-start(), calls=%async_computation.5 | async-start | bytes 11141120 | tf_op jit(solution)/shard_map/all_gather | solution.py:24
  90.9 179.8 %all-gather.7.cloned.1.call-start = ((), (), s32[]{:S(2)}) async-start(), calls=%async_computation.6 | async-start | bytes 5570560 | tf_op jit(solution)/shard_map/all_gather | solution.py:82
  161.1 3.5 copy-start.8
  162.3 2.3 copy-start.3
  184.2 127.9 %all-to-all-start.2 = ((bf16[8,16,32,640]{3,2,1,0:T(8,128)(2,1)}), bf16[8,16,32,640]{3,2,1,0:T(8,128)(2,1)}, u32[]{:S(2)}, u32[]{:S(2)}) async-start(bf16[8,16,32,640]{3,2,1,0:T(8,128)(2,1)} %bitcast.63), calls=%async_computation.2 | async-start | bytes 10485760 | tf_op jit(solution)/shard_map/all_to_all | solution.py:38
  190.4 140.5 %reduce-scatter.4.cloned.1.call-start = ((), (), s32[]{:S(2)}) async-start(), calls=%async_computation.8 | async-start | bytes 1474560
  315.6 1.1 copy-start.2
  316.6 29.3 %copy-start.1 = (bf16[256,5120]{1,0:T(8,128)(2,1)S(1)}, bf16[256,5120]{1,0:T(8,128)(2,1)}, u32[]{:S(2)}) copy-start(bf16[256,5120]{1,0:T(8,128)(2,1)} %param.14) | copy-start | bytes 7864324
  316.7 4.7 %collective-permute-start.1 = (bf16[16,32,640]{2,1,0:T(8,128)(2,1)S(1)}, bf16[16,32,640]{2,1,0:T(8,128)(2,1)}, u32[]{:S(2)}, u32[]{:S(2)}) collective-permute-start(bf16[16,32,640]{2,1,0:T(8,128)(2,1)S(1)} %convert_element_type.53), channel_id=1, source_target_pairs={{0,8},{8,0},{16,24},{24,16},{32,40},{40,32},{48,56},{56,48},{64,72... | collective-permute-start | bytes 1966088 | tf_op jit(solution)/shard_map/ppermute | solution.py:45
  323.4 20.4 %all-to-all-start.3 = ((bf16[16,16,640]{2,1,0:T(8,128)(2,1)}), bf16[16,16,640]{2,1,0:T(8,128)(2,1)S(1)}, u32[]{:S(2)}, u32[]{:S(2)}) async-start(bf16[16,16,640]{2,1,0:T(8,128)(2,1)} %fusion.20), calls=%async_computation.3 | async-start | bytes 655360 | tf_op jit(solution)/shard_map/all_to_all | solution.py:113
Sparse Core Ops, SparseCore 0:
  89.0 66.6 all-gather.8
  157.5 68.1 all-gather.4
  227.5 43.2 all-gather.6
  282.5 41.4 reduce-scatter.3
